TPU v7x, 32 devices: a whole 2x2x4 slice. The times are simulated.
32 devices in a mesh: rep: 4 (over y, x), shard: 4 (over z), tp: 2 (over core).
Axes of the slice: x: 2, y: 2, z: 4, core: 2. Of those that a mesh axis runs over, the one named last changes fastest.
Arguments:
- x_in: bfloat16 [4, 1536, 1536], P('rep', 'shard'), may hold values from -6 to 6
- query_key_value_weight: bfloat16 [2, 1536, 2048], P(None, 'shard', 'tp'), may hold values from -0.15625 to 0.15625
- qkv_bias: bfloat16 [2, 2048], P(None, 'tp'), may hold values from -3 to 3
- output_weight: bfloat16 [2, 1536, 1536], P(None, 'shard', 'tp'), may hold values from -0.875 to 0.875
- feedforward_entry_matrix: bfloat16 [2, 1536, 2, 8960], P(None, 'shard', None, 'tp'), may hold values from -0.15625 to 0.15625
- down_weight: bfloat16 [2, 1536, 8960], P(None, 'shard', 'tp'), may hold values from -0.125 to 0.125
- norm_gains: bfloat16 [2, 2, 1536], replicated, may hold values from 0.5 to 1.5
- piece_starts: int32 [4, 2], P('rep'), may hold values from 0 to 1280, as said below
- seq_lengths: int32 [4], P('rep'), may hold values from 1 to 1536, 4608 in all
- grad_out: bfloat16 [4, 1536, 1536], P('rep', 'shard'), may hold values from -6 to 6
Outputs:
- out_act: bfloat16 [4, 1536, 1536], P('rep', 'shard')
- grad_input: float32 [4, 1536, 1536], P('rep', 'shard')
- grad_qkv: float32 [2, 1536, 2048], P(None, 'shard', 'tp')
- grad_bias: float32 [2, 2048], P(None, 'tp')
- grad_out_proj: float32 [2, 1536, 1536], P(None, 'shard', 'tp')
- grad_gate_up: float32 [2, 1536, 2, 8960], P(None, 'shard', None, 'tp')
- grad_down: float32 [2, 1536, 8960], P(None, 'shard', 'tp')
- grad_gains: float32 [2, 2, 1536], replicated
Inputs may be any that keep to these rules, and one draw needn't show every extreme that they name: `piece_starts`: piece k of a sequence starts between k * 768 and (k + 1) * 768 - 256, so pieces never intersect.
All inputs are finite; a program needn't handle non-finite values. No bound on the sum of `seq_lengths` on one device may be relied on, other than what follows from the above.
Results may differ from a plain program's by a relative error of at most 0.017.
Values may be sent and summed in bfloat16 or wider, within the bound.
A program may use at most 512 MiB of HBM per device.

v0:
```python
import math

import jax
import jax.numpy as jnp
from jax import lax
from jax.sharding import PartitionSpec as P

QUERY_HEADS = 12
KEY_VALUE_HEADS = 2
HEAD_SIZE = 128
LAYERS = 2
PIECE = 256
PIECES = 2


EPS = 1e-06
THETA = 1000000.0


def rope_tables(positions):
    freq = jnp.exp(
        jnp.arange(HEAD_SIZE // 2, dtype=jnp.float32) * (-2.0 * math.log(THETA) / HEAD_SIZE)
    )
    angle = positions.astype(jnp.float32)[:, None] * freq[None, :]
    angle = jnp.concatenate([angle, angle], axis=1)
    return (jnp.cos(angle), jnp.sin(angle))


def rotate(content_entries, cosine, sine):
    half = content_entries.shape[-1] // 2
    turned = jnp.concatenate([-content_entries[..., half:], content_entries[..., :half]], axis=-1)
    return content_entries * cosine + turned * sine


def rotate_back(grads, cosine, sine):
    half = grads.shape[-1] // 2
    shifted = grads * sine
    return grads * cosine + jnp.concatenate([shifted[..., half:], -shifted[..., :half]], axis=-1)


def piece_ids(positions, starts):
    inside = (positions[..., :, None] >= starts[..., None, :]) & (
        positions[..., :, None] < starts[..., None, :] + PIECE
    )
    labels = jnp.arange(1, PIECES + 1, dtype=jnp.int32)
    return jnp.sum(jnp.where(inside, labels, 0), axis=-1)


def norm_scale(content_entries):
    return lax.rsqrt(jnp.mean(content_entries * content_entries, axis=-1, keepdims=True) + EPS)


def norm_back(content_entries, scale, gain, grad_normed):
    inner = jnp.mean(grad_normed * gain * content_entries, axis=-1, keepdims=True)
    grad_values = scale * gain * grad_normed - content_entries * (scale * scale * scale) * inner
    gain_grad = jnp.sum(grad_normed * content_entries * scale, axis=0)
    return (grad_values, gain_grad)


def masked_scores(query_rows, keys_all, seen, root):
    raw = (
        jnp.einsum("sqgjd,skgd->sgjqk", query_rows, keys_all, preferred_element_type=jnp.float32)
        / root
    )
    return jnp.where(seen[:, None, None], raw, -1e30)


def weight_terms(operands):
    parts = []
    for left, right in operands:
        parts.append(
            lax.dot_general(
                left, right, (((0,), (0,)), ((), ())), preferred_element_type=jnp.float32
            )
        )
    return jnp.concatenate(parts, axis=1)


def right_product(left, right):
    return lax.dot_general(
        left, right, (((1,), (1,)), ((), ())), preferred_element_type=jnp.float32
    )


def body(
    x_in,
    query_key_value_weight,
    qkv_bias,
    output_weight,
    feedforward_entry_matrix,
    down_weight,
    norm_gains,
    piece_starts,
    seq_lengths,
    grad_out,
):
    seqs, span, width = x_in.shape
    shards = lax.axis_size("shard")
    place = lax.axis_index("shard")
    length = span * shards
    rows = seqs * span
    group_index = QUERY_HEADS // KEY_VALUE_HEADS
    joined_width = query_key_value_weight.shape[2]
    local_groups = joined_width // ((group_index + 2) * HEAD_SIZE)
    heads_width = output_weight.shape[2]
    hidden_width = down_weight.shape[2]
    root = math.sqrt(HEAD_SIZE)
    own_pos = place * span + jnp.arange(span, dtype=jnp.int32)
    all_pos = jnp.arange(length, dtype=jnp.int32)
    cosine, sine = rope_tables(own_pos)
    cos_query = cosine[None, :, None, None, :]
    sin_query = sine[None, :, None, None, :]
    cos_key = cosine[None, :, None, :]
    sin_key = sine[None, :, None, :]
    own_ids = piece_ids(jnp.broadcast_to(own_pos, (seqs, span)), piece_starts)
    all_ids = piece_ids(jnp.broadcast_to(all_pos, (seqs, length)), piece_starts)
    same_piece = (own_ids[:, :, None] == all_ids[:, None, :]) & (own_ids[:, :, None] > 0)
    seen = (all_pos[None, None, :] < seq_lengths[:, None, None]) & (
        (all_pos[None, None, :] <= own_pos[None, :, None]) | same_piece
    )
    residual_state = x_in.astype(jnp.float32).reshape(rows, width)
    saved = []
    for index in range(LAYERS):
        gathered = (
            lax.all_gather(query_key_value_weight[index], "shard", axis=0, tiled=True),
            lax.all_gather(output_weight[index], "shard", axis=0, tiled=True),
            lax.all_gather(feedforward_entry_matrix[index], "shard", axis=0, tiled=True),
            lax.all_gather(down_weight[index], "shard", axis=0, tiled=True),
        )
        full_qkv, full_out, full_gate_up, full_down = gathered
        gains = norm_gains[index].astype(jnp.float32)
        scale_one = norm_scale(residual_state)
        first_normed = (residual_state * scale_one * gains[0]).astype(jnp.bfloat16)
        joined_output = jnp.dot(
            first_normed, full_qkv, preferred_element_type=jnp.float32
        ) + qkv_bias[index].astype(jnp.float32)
        joined_output = joined_output.reshape(seqs, span, local_groups, group_index + 2, HEAD_SIZE)
        query_rows = rotate(joined_output[:, :, :, :group_index], cos_query, sin_query).astype(
            jnp.bfloat16
        )
        keys = rotate(joined_output[:, :, :, group_index], cos_key, sin_key).astype(jnp.bfloat16)
        content_entries = joined_output[:, :, :, group_index + 1].astype(jnp.bfloat16)
        keys_all, values_all = (
            lax.all_gather(keys, "shard", axis=1, tiled=True),
            lax.all_gather(content_entries, "shard", axis=1, tiled=True),
        )
        attention_logits = masked_scores(query_rows, keys_all, seen, root)
        log_total = jax.nn.logsumexp(attention_logits, axis=-1, keepdims=True)
        shares = jnp.exp(attention_logits - log_total).astype(jnp.bfloat16)
        mixed_output = jnp.einsum(
            "sgjqk,skgd->sqgjd", shares, values_all, preferred_element_type=jnp.float32
        )
        mixed_output = mixed_output.astype(jnp.bfloat16).reshape(rows, heads_width)
        middle_state = residual_state + lax.psum(right_product(mixed_output, full_out), "tp")
        scale_two = norm_scale(middle_state)
        rescaled_after_attention = (middle_state * scale_two * gains[1]).astype(jnp.bfloat16)
        swiglu_input_pair = jnp.einsum(
            "rd,dcf->rcf",
            rescaled_after_attention,
            full_gate_up,
            preferred_element_type=jnp.float32,
        )
        hidden_state = (jax.nn.silu(swiglu_input_pair[:, 0]) * swiglu_input_pair[:, 1]).astype(
            jnp.bfloat16
        )
        kept = None
        saved.append(
            (
                residual_state,
                scale_one,
                first_normed,
                query_rows,
                keys_all,
                values_all,
                log_total,
                mixed_output,
                middle_state,
                scale_two,
                rescaled_after_attention,
                swiglu_input_pair,
                hidden_state,
                kept,
            )
        )
        residual_state = middle_state + lax.psum(right_product(hidden_state, full_down), "tp")
    out_act = residual_state.astype(jnp.bfloat16).reshape(seqs, span, width)
    flow = grad_out.astype(jnp.float32).reshape(rows, width)
    pieces = [None] * LAYERS
    gain_grads = [None] * LAYERS
    bias_grads = [None] * LAYERS
    for index in reversed(range(LAYERS)):
        (
            residual_state,
            scale_one,
            first_normed,
            query_rows,
            keys_all,
            values_all,
            log_total,
            mixed_output,
            middle_state,
            scale_two,
            rescaled_after_attention,
            swiglu_input_pair,
            hidden_state,
            kept,
        ) = saved[index]
        full_qkv, full_out, full_gate_up, full_down = (
            lax.all_gather(query_key_value_weight[index], "shard", axis=0, tiled=True),
            lax.all_gather(output_weight[index], "shard", axis=0, tiled=True),
            lax.all_gather(feedforward_entry_matrix[index], "shard", axis=0, tiled=True),
            lax.all_gather(down_weight[index], "shard", axis=0, tiled=True),
        )
        gains = norm_gains[index].astype(jnp.float32)
        down_grad = flow.astype(jnp.bfloat16)
        hidden_grad = jnp.dot(down_grad, full_down, preferred_element_type=jnp.float32)
        gate = swiglu_input_pair[:, 0]
        upper = swiglu_input_pair[:, 1]
        sigmoid = jax.nn.sigmoid(gate)
        gate_grad = hidden_grad * upper * (sigmoid + gate * sigmoid * (1.0 - sigmoid))
        up_grad = hidden_grad * (gate * sigmoid)
        gate_up_grad = jnp.stack([gate_grad, up_grad], axis=1).astype(jnp.bfloat16)
        normed_two_part = jnp.einsum(
            "rcf,dcf->rd", gate_up_grad, full_gate_up, preferred_element_type=jnp.float32
        )
        normed_two_grad = lax.psum(normed_two_part, "tp")
        middle_grad, gain_two = norm_back(middle_state, scale_two, gains[1], normed_two_grad)
        middle_grad = flow + middle_grad
        out_grad = middle_grad.astype(jnp.bfloat16)
        mixed_grad = jnp.dot(out_grad, full_out, preferred_element_type=jnp.float32).astype(
            jnp.bfloat16
        )
        mixed_grad = mixed_grad.reshape(seqs, span, local_groups, group_index, HEAD_SIZE)
        attention_logits = masked_scores(query_rows, keys_all, seen, root)
        exact = jnp.exp(attention_logits - log_total)
        shares = exact.astype(jnp.bfloat16)
        share_grad = jnp.einsum(
            "sqgjd,skgd->sgjqk", mixed_grad, values_all, preferred_element_type=jnp.float32
        )
        centre = jnp.sum(exact * share_grad, axis=-1, keepdims=True)
        score_grad = (exact * (share_grad - centre)).astype(jnp.bfloat16)
        query_grad = (
            jnp.einsum(
                "sgjqk,skgd->sqgjd", score_grad, keys_all, preferred_element_type=jnp.float32
            )
            / root
        )
        key_grad = (
            jnp.einsum(
                "sgjqk,sqgjd->skgd", score_grad, query_rows, preferred_element_type=jnp.float32
            )
            / root
        )
        value_grad = jnp.einsum(
            "sgjqk,sqgjd->skgd", shares, mixed_grad, preferred_element_type=jnp.float32
        )
        key_own, value_own = (
            lax.psum_scatter(
                key_grad.astype(jnp.bfloat16), "shard", scatter_dimension=1, tiled=True
            ).astype(jnp.float32),
            lax.psum_scatter(
                value_grad.astype(jnp.bfloat16), "shard", scatter_dimension=1, tiled=True
            ).astype(jnp.float32),
        )
        unrotated_asks = rotate_back(query_grad, cos_query, sin_query)
        key_raw = rotate_back(key_own, cos_key, sin_key)
        joined_grad = jnp.concatenate(
            [unrotated_asks, key_raw[:, :, :, None], value_own[:, :, :, None]], axis=3
        )
        joined_grad = joined_grad.reshape(rows, joined_width).astype(jnp.bfloat16)
        bias_grads[index] = jnp.sum(joined_grad, axis=0, dtype=jnp.float32)
        normed_one_grad = lax.psum(
            right_product(joined_grad, full_qkv).astype(jnp.bfloat16), "tp"
        ).astype(jnp.float32)
        input_grad, gain_one = norm_back(residual_state, scale_one, gains[0], normed_one_grad)
        gain_grads[index] = jnp.stack([gain_one, gain_two])
        flow = middle_grad + input_grad
        pairs = (
            (first_normed, joined_grad),
            (out_grad, mixed_output),
            (rescaled_after_attention, gate_up_grad.reshape(rows, 2 * hidden_width)),
            (down_grad, hidden_state),
        )
        pieces[index] = lax.psum_scatter(
            weight_terms(pairs).astype(jnp.bfloat16), "shard", scatter_dimension=0, tiled=True
        ).astype(jnp.float32)
    stacked = jnp.stack(pieces)
    summed = lax.psum(stacked.astype(jnp.bfloat16), "rep").astype(jnp.float32)
    gains_total, bias_total = lax.psum(
        (jnp.stack(gain_grads), jnp.stack(bias_grads)), ("rep", "shard")
    )
    second = joined_width + heads_width
    third = second + 2 * hidden_width
    grad_qkv = summed[:, :, :joined_width]
    grad_out_proj = summed[:, :, joined_width:second]
    grad_gate_up = summed[:, :, second:third].reshape(LAYERS, summed.shape[1], 2, hidden_width)
    grad_down = summed[:, :, third:]
    grad_input = flow.reshape(seqs, span, width)
    return (
        out_act,
        grad_input,
        grad_qkv,
        bias_total,
        grad_out_proj,
        grad_gate_up,
        grad_down,
        gains_total,
    )


def solution(mesh):
    return jax.shard_map(
        body,
        mesh=mesh,
        in_specs=(
            P("rep", "shard", None),
            P(None, "shard", "tp"),
            P(None, "tp"),
            P(None, "shard", "tp"),
            P(None, "shard", None, "tp"),
            P(None, "shard", "tp"),
            P(),
            P("rep", None),
            P("rep"),
            P("rep", "shard", None),
        ),
        out_specs=(
            P("rep", "shard", None),
            P("rep", "shard", None),
            P(None, "shard", "tp"),
            P(None, "tp"),
            P(None, "shard", "tp"),
            P(None, "shard", None, "tp"),
            P(None, "shard", "tp"),
            P(),
        ),
        check_vma=False,
    )
```

profile of v0, /device:TPU:0, one launch (start us, length us, event | category | flops | bytes accessed | tf_op | source)
XLA Modules:
  0.0 4123.2 jit_solution(10268085395848394974)
XLA Ops:
  18.9 57.5 %all-gather.19.cloned.1.call-done = bf16[1,1536,1024]{2,1,0:T(8,128)(2,1)} async-done(((bf16[1,384,1024]{2,1,0:T(8,128)(2,1)}), bf16[1,1536,1024]{2,1,0:T(8,128)(2,1)}) %all-gather.19.cloned.1.call-update) | async-done | bytes 3145744 | tf_op jit(solution)/shard_map/all_gather | solution.py:125
  82.6 18.9 all-gather.1
  110.0 18.5 all_gather.46
  145.3 11.9 fusion.177
  161.0 7.0 fusion.178
  171.9 461.1 %all-gather.23.cloned.1.call-done = bf16[1,1536,2,4480]{3,1,2,0:T(8,128)(2,1)} async-done(((bf16[1,384,2,4480]{3,1,2,0:T(8,128)(2,1)}), bf16[1,1536,2,4480]{3,1,2,0:T(8,128)(2,1)}) %all-gather.23.cloned.1.call-update) | async-done | bytes 27525136 | tf_op jit(solution)/shard_map/all_gather | solution.py:127
  633.0 19.2 fusion.6
  652.2 7.1 multiply_convert_fusion.1
  659.4 211.3 %all-gather.25.cloned.1.call-done = bf16[1,1536,4480]{2,1,0:T(8,128)(2,1)} async-done(((bf16[1,384,4480]{2,1,0:T(8,128)(2,1)}), bf16[1,1536,4480]{2,1,0:T(8,128)(2,1)}) %all-gather.25.cloned.1.call-update) | async-done | bytes 13762576 | tf_op jit(solution)/shard_map/all_gather | solution.py:128
  870.7 10.8 fusion.21
  883.1 18.5 all-reduce.13.cloned.1.call-done
  905.5 62.9 %all-gather.27.cloned.1.call-done = bf16[1,1536,1024]{2,1,0:T(8,128)(2,1)} async-done(((bf16[1,384,1024]{2,1,0:T(8,128)(2,1)}), bf16[1,1536,1024]{2,1,0:T(8,128)(2,1)}) %all-gather.27.cloned.1.call-update) | async-done | bytes 3145744 | tf_op jit(solution)/shard_map/all_gather | solution.py:125
  975.9 19.0 all-gather.6
  995.7 18.9 all_gather.52
  1035.2 6.8 copy.216
  1043.0 13.2 all-reduce.15.cloned.1.call-done
  1058.9 462.7 %all-gather.31.cloned.1.call-done = bf16[1,1536,2,4480]{3,1,2,0:T(8,128)(2,1)} async-done(((bf16[1,384,2,4480]{3,1,2,0:T(8,128)(2,1)}), bf16[1,1536,2,4480]{3,1,2,0:T(8,128)(2,1)}) %all-gather.31.cloned.1.call-update) | async-done | bytes 27525136 | tf_op jit(solution)/shard_map/all_gather | solution.py:127
  1521.6 19.3 fusion.2
  1540.9 218.0 %all-gather.33.cloned.1.call-done = bf16[1,1536,4480]{2,1,0:T(8,128)(2,1)} async-done(((bf16[1,384,4480]{2,1,0:T(8,128)(2,1)}), bf16[1,1536,4480]{2,1,0:T(8,128)(2,1)}) %all-gather.33.cloned.1.call-update) | async-done | bytes 13762576 | tf_op jit(solution)/shard_map/all_gather | solution.py:128
  1758.9 14.3 fusion.31
  1773.2 17.9 fusion.49
  1798.8 10.2 copy.178
  1819.5 8.3 fusion.99
  1827.8 9.2 fusion.12
  1842.0 10.2 fusion.27
  1865.2 20.6 reduce-scatter.11.cloned.1.call-done
  1896.0 17.9 fusion.17
  1919.6 15.7 multiply_bitcast_fusion.1
  1935.3 18.1 fusion.46
  1954.6 15.7 fusion.8
  1970.3 22.2 convolution_convert_fusion
  2007.5 7.6 fusion.97
  2015.1 9.9 fusion.9
  2026.4 10.2 fusion.28
  2042.4 31.3 pad_maximum_fusion.1
  2074.2 6.6 maximum_convert_fusion.1
  2080.8 10.3 copy.173
  2091.1 13.1 convolution_convert_fusion.3
  2104.2 21.9 convolution_convert_fusion.1
  2151.5 31.4 pad_maximum_fusion
  2188.4 651.8 %reduce-scatter.17.cloned.1.call-done = bf16[384,15232]{1,0:T(8,128)(2,1)} async-done(((bf16[1536,15232]{1,0:T(8,128)(2,1)}), bf16[384,15232]{1,0:T(8,128)(2,1)}) %reduce-scatter.17.cloned.1.call-update) | async-done | bytes 11698192 | tf_op jit(solution)/shard_map/reduce_scatter | solution.py:284
  2840.2 769.5 %reduce-scatter.15.cloned.1.call-done = bf16[384,15232]{1,0:T(8,128)(2,1)} async-done(((bf16[1536,15232]{1,0:T(8,128)(2,1)}), bf16[384,15232]{1,0:T(8,128)(2,1)}) %reduce-scatter.15.cloned.1.call-update) | async-done | bytes 11698192 | tf_op jit(solution)/shard_map/reduce_scatter | solution.py:284
  3609.7 17.2 pad_maximum_fusion.2
  3638.7 79.7 %all-reduce = (f32[2,1024]{1,0:T(2,128)}, f32[2,2,1536]{2,1,0:T(2,128)}) all-reduce(f32[2,1024]{1,0:T(2,128)S(1)} %pad_maximum_fusion.6, f32[2,2,1536]{2,1,0:T(2,128)} %pad_maximum_fusion.5), channel_id=1, replica_groups=mesh['rep'=4,'shard'=4,'tp'=2] {'rep','shard'}, use_global_device_ids=true, to_apply=%region_33.34 | all-reduce | flops 8192 | bytes 65536 | tf_op jit(solution)/shard_map/psum | solution.py:289
  3722.5 331.8 %all-reduce.23.cloned.1.call-done = bf16[2,384,15232]{2,1,0:T(8,128)(2,1)} async-done(((bf16[2,384,15232]{2,1,0:T(8,128)(2,1)}), bf16[2,384,15232]{2,1,0:T(8,128)(2,1)}) %all-reduce.23.cloned.1.call-update) | async-done | bytes 23396368 | tf_op jit(solution)/shard_map/psum | solution.py:288
  4054.3 15.5 slice.244
  4069.8 31.1 reshape.1172
  4107.2 9.0 slice.245
  (344 shorter events, 216.3 us)
Async XLA Ops:
  7.2 69.2 %all-gather.19.cloned.1.call-start = ((), (), s32[]{:S(2)}) async-start(), calls=%async_computation.17 | async-start | bytes 3932160 | tf_op jit(solution)/shard_map/all_gather | solution.py:125
  10.1 130.8 %all-gather.21.cloned.1.call-start = ((), (), s32[]{:S(2)}) async-start(), calls=%async_computation.18 | async-start | bytes 2949120 | tf_op jit(solution)/shard_map/all_gather | solution.py:126
  11.2 157.0 %all-reduce.11.cloned.1.call-start = ((), (), s32[]{:S(2)}) async-start(), calls=%async_computation.6 | async-start | bytes 4718592 | tf_op jit(solution)/shard_map/psum | solution.py:154
  13.1 66.6 %copy-start.69 = (f32[384]{0:T(512)}, f32[384]{0:T(512)S(1)}, u32[]{:S(2)}) copy-start(f32[384]{0:T(512)S(1)} %get-tuple-element.73) | copy-start | bytes 4612
  13.8 65.9 %copy-start.65 = (f32[1536]{0:T(1024)}, f32[1536]{0:T(1024)S(1)}, u32[]{:S(2)}) copy-start(f32[1536]{0:T(1024)S(1)} %get-tuple-element.19) | copy-start | bytes 18436
  13.8 619.2 %copy-start.56 = (f32[1536]{0:T(1024)}, f32[1536]{0:T(1024)S(1)}, u32[]{:S(2)}) copy-start(f32[1536]{0:T(1024)S(1)} %get-tuple-element.18) | copy-start | bytes 18436
  13.9 95.2 %copy-start.18 = (f32[1,384,1,64]{3,1,2,0:T(8,128)}, f32[1,384,1,64]{3,1,2,0:T(8,128)S(1)}, u32[]{:S(2)}) copy-start(f32[1,384,1,64]{3,1,2,0:T(8,128)S(1)} %get-tuple-element.70) | copy-start | bytes 294916
  105.7 22.7 copy-start.31
  105.7 22.7 copy-start.42
  105.7 22.7 copy-start.44
  109.0 21.0 copy-start.16
  145.2 487.8 %all-gather.23.cloned.1.call-start = ((), (), s32[]{:S(2)}) async-start(), calls=%async_computation.19 | async-start | bytes 34406400 | tf_op jit(solution)/shard_map/all_gather | solution.py:127
  160.9 709.8 %all-gather.25.cloned.1.call-start = ((), (), s32[]{:S(2)}) async-start(), calls=%async_computation.20 | async-start | bytes 17203200 | tf_op jit(solution)/shard_map/all_gather | solution.py:128
  167.9 733.7 %all-reduce.13.cloned.1.call-start = ((), (), s32[]{:S(2)}) async-start(), calls=%async_computation.7 | async-start | bytes 4718592 | tf_op jit(solution)/shard_map/psum | solution.py:185
  171.2 730.4 %copy-start.4 = (f32[384,1536]{1,0:T(8,128)}, f32[384,1536]{1,0:T(8,128)S(1)}, u32[]{:S(2)}) copy-start(f32[384,1536]{1,0:T(8,128)S(1)} %get-tuple-element.33) | copy-start | bytes 7077892
  171.9 480.4 %copy-start.60 = (f32[384]{0:T(512)}, f32[384]{0:T(512)S(1)}, u32[]{:S(2)}) copy-start(f32[384]{0:T(512)S(1)} %get-tuple-element.75) | copy-start | bytes 4612
  881.5 86.9 %all-gather.27.cloned.1.call-start = ((), (), s32[]{:S(2)}) async-start(), calls=%async_computation.21 | async-start | bytes 3932160 | tf_op jit(solution)/shard_map/all_gather | solution.py:125
  882.3 148.5 %all-gather.29.cloned.1.call-start = ((), (), s32[]{:S(2)}) async-start(), calls=%async_computation.22 | async-start | bytes 2949120 | tf_op jit(solution)/shard_map/all_gather | solution.py:126
  883.0 173.2 %all-reduce.15.cloned.1.call-start = ((), (), s32[]{:S(2)}) async-start(), calls=%async_computation.8 | async-start | bytes 4718592 | tf_op jit(solution)/shard_map/psum | solution.py:154
  883.1 85.3 %copy-start.62 = (f32[1536]{0:T(1024)}, f32[1536]{0:T(1024)S(1)}, u32[]{:S(2)}) copy-start(f32[1536]{0:T(1024)S(1)} %get-tuple-element.17) | copy-start | bytes 18436
  905.5 68.1 %copy-start.71 = (f32[384]{0:T(512)}, f32[384]{0:T(512)S(1)}, u32[]{:S(2)}) copy-start(f32[384]{0:T(512)S(1)} %get-tuple-element.77) | copy-start | bytes 4612
  973.6 21.2 copy-start.19
  975.5 39.1 copy-start.43
  975.6 39.1 copy-start.45
  995.7 19.2 copy-start.17
  1035.2 486.4 %all-gather.31.cloned.1.call-start = ((), (), s32[]{:S(2)}) async-start(), calls=%async_computation.23 | async-start | bytes 34406400 | tf_op jit(solution)/shard_map/all_gather | solution.py:127
  1042.0 716.8 %all-gather.33.cloned.1.call-start = ((), (), s32[]{:S(2)}) async-start(), calls=%async_computation.24 | async-start | bytes 17203200 | tf_op jit(solution)/shard_map/all_gather | solution.py:128
  1042.8 768.4 %all-reduce.17.cloned.1.call-start = ((), (), s32[]{:S(2)}) async-start(), calls=%async_computation.9 | async-start | bytes 4718592 | tf_op jit(solution)/shard_map/psum | solution.py:226
  1058.9 911.4 %copy-start.6 = (f32[384,1536]{1,0:T(8,128)}, f32[384,1536]{1,0:T(8,128)S(1)}, u32[]{:S(2)}) copy-start(f32[384,1536]{1,0:T(8,128)S(1)} %get-tuple-element.29) | copy-start | bytes 7077892
  1773.1 18.2 copy-start.55
  1773.2 18.3 copy-start.54
  1791.1 73.0 %reduce-scatter.19.cloned.1.call-start = ((), (), s32[]{:S(2)}) async-start(), calls=%async_computation.25 | async-start | bytes 491520
  1791.5 70.9 %copy-start.40 = (f32[384,128]{0,1:T(8,128)}, f32[384,128]{0,1:T(8,128)S(1)}, u32[]{:S(2)}) copy-start(f32[384,128]{0,1:T(8,128)S(1)} %copy.158) | copy-start | bytes 589828
  1842.0 43.9 %reduce-scatter.11.cloned.1.call-start = ((), (), s32[]{:S(2)}) async-start(), calls=%async_computation.10 | async-start | bytes 491520 | tf_op jit(solution)/shard_map/reduce_scatter | solution.py:258
  1858.0 55.9 %all-reduce.19.cloned.1.call-start = ((), (), s32[]{:S(2)}) async-start(), calls=%async_computation.11 | async-start | bytes 2359296 | tf_op jit(solution)/shard_map/psum | solution.py:272
  1895.5 18.4 copy-start.63
  1895.5 18.4 copy-start.72
  1895.5 105.4 %all-reduce.25.cloned.1.call-start = ((), (), s32[]{:S(2)}) async-start(), calls=%async_computation.27 | async-start | bytes 9437184 | tf_op jit(solution)/shard_map/psum | solution.py:185
  1919.6 15.7 copy-start.23
  1953.4 183.1 %reduce-scatter.21.cloned.1.call-start = ((), (), s32[]{:S(2)}) async-start(), calls=%async_computation.26 | async-start | bytes 491520
  1970.3 22.2 copy-start.39
  2026.4 111.4 %reduce-scatter.13.cloned.1.call-start = ((), (), s32[]{:S(2)}) async-start(), calls=%async_computation.12 | async-start | bytes 491520 | tf_op jit(solution)/shard_map/reduce_scatter | solution.py:258
  2042.4 797.8 %reduce-scatter.17.cloned.1.call-start = ((), (), s32[]{:S(2)}) async-start(), calls=%async_computation.15 | async-start | bytes 58490880 | tf_op jit(solution)/shard_map/reduce_scatter | solution.py:284
  2073.8 1535.9 %reduce-scatter.15.cloned.1.call-start = ((), (), s32[]{:S(2)}) async-start(), calls=%async_computation.14 | async-start | bytes 58490880 | tf_op jit(solution)/shard_map/reduce_scatter | solution.py:284
  2104.2 21.9 copy-start.38
  2182.9 1451.1 %all-reduce.21.cloned.1.call-start = ((), (), s32[]{:S(2)}) async-start(), calls=%async_computation.13 | async-start | bytes 2359296 | tf_op jit(solution)/shard_map/psum | solution.py:272
  2188.4 1865.9 %all-reduce.23.cloned.1.call-start = ((), (), s32[]{:S(2)}) async-start(), calls=%async_computation.16 | async-start | bytes 46792704 | tf_op jit(solution)/shard_map/psum | solution.py:288
  3633.4 85.8 %copy-start.12 = (f32[384,1536]{1,0:T(8,128)S(1)}, f32[384,1536]{1,0:T(8,128)}, u32[]{:S(2)}) copy-start(f32[384,1536]{1,0:T(8,128)} %copy-done.11) | copy-start | bytes 7077892
  (56 other events, 223.1 us)
Sparse Core Ops, SparseCore 0:
  10.2 66.1 all-gather.18
  78.5 59.9 all-gather.20
  145.4 21.6 all-reduce.10
  169.0 463.9 all-gather.22
  635.0 235.6 all-gather.24
  881.6 19.9 all-reduce.12
  903.8 64.6 all-gather.26
  970.0 60.7 all-gather.28
  1035.3 20.8 all-reduce.14
  1057.6 463.9 all-gather.30
  1523.2 235.6 all-gather.32
  1791.2 19.9 all-reduce.16
  1842.1 21.9 reduce-scatter.18
  1866.8 18.9 reduce-scatter.10
  1895.6 17.8 all-reduce.18
  1953.5 29.7 all-reduce.24
  2026.5 21.5 reduce-scatter.20
  2050.3 19.1 reduce-scatter.12
  2073.9 766.2 reduce-scatter.16
  2842.4 767.2 reduce-scatter.14
  3612.6 21.3 all-reduce.20
  3638.2 416.0 all-reduce.22
where the time goes:
time: 4130 us; the launch traced here: 4120 us
  waiting for transfers between devices  3290 us (80%)
  matrix products  311 us (8%)
  other arithmetic  179 us (4%)
  local copies, waits for them, and re-layouts  170 us (4%)
  blocking collectives  155 us (4%)
    reduce_scatter x2, waiting for transfers between devices, body(): lax.psum_scatter(weight_terms(pairs).astype(jnp.bfloat16), 'shard', scatt...  1420 us
    all_gather x2, waiting for transfers between devices, body(): lax.all_gather(feedforward_entry_matrix[index], 'shard', axis=0, tiled=True)  924 us
    all_gather x2, waiting for transfers between devices, body(): lax.all_gather(down_weight[index], 'shard', axis=0, tiled=True)  429 us
    psum x1, waiting for transfers between devices, body(): summed = lax.psum(stacked.astype(jnp.bfloat16), 'rep').astype(jnp.float32)  332 us
    all_gather x2, waiting for transfers between devices, body(): lax.all_gather(query_key_value_weight[index], 'shard', axis=0, tiled=True)  120 us
    dot_general x8, matrix products, weight_terms(): lax.dot_general(left, right, (((0,), (0,)), ((), ())), preferred_element_...  87.8 us
  transfers between devices with their start and end apart: 22, of which 16 were waited for; matrix products, arithmetic and copies ran while one was open for 10% of the time, Pallas kernels for 0%

commit v1 on v0

--- a/solution.py
+++ b/solution.py
@@ -11,6 +11,7 @@
 LAYERS = 2
 PIECE = 256
 PIECES = 2
+LANES = 128
 
 
 EPS = 1e-06
@@ -65,15 +66,54 @@
     return jnp.where(seen[:, None, None], raw, -1e30)
 
 
-def weight_terms(operands):
+def left_product(left, right):
+    return lax.dot_general(
+        left, right, (((0,), (0,)), ((), ())), preferred_element_type=jnp.float32
+    ).astype(jnp.bfloat16)
+
+
+def layer_weights(qkv, out, gate_up, down, first_unit, block):
+    depth = qkv.shape[0]
+    part = depth // lax.axis_size("rep")
+    first_row = lax.axis_index("rep") * part
+
+    def whole(weight):
+        rows = lax.dynamic_slice_in_dim(weight, first_row, part, axis=0)
+        return lax.all_gather(rows, ("shard", "rep"), axis=0, tiled=True)
+
+    gate_up_block = lax.dynamic_slice_in_dim(gate_up, first_unit, block, axis=2)
+    down_block = lax.dynamic_slice_in_dim(down, first_unit, block, axis=1)
+    return (
+        whole(qkv),
+        whole(out),
+        lax.all_gather(gate_up_block.reshape(depth, 2 * block), "shard", axis=0, tiled=True),
+        lax.all_gather(down_block, "shard", axis=0, tiled=True),
+    )
+
+
+def plane_sum(terms):
+    part = lax.psum_scatter(terms.astype(jnp.bfloat16), "rep", scatter_dimension=0, tiled=True)
+    return lax.psum(part, "tp").astype(jnp.float32)
+
+
+def spread_block(grad):
+    part = lax.psum_scatter(grad, "shard", scatter_dimension=0, tiled=True)
+    return lax.all_gather(part, "rep", axis=0, tiled=False)
+
+
+def join_blocks(blocks, width):
+    reps, block = blocks.shape[0], blocks.shape[-1]
     parts = []
-    for left, right in operands:
-        parts.append(
-            lax.dot_general(
-                left, right, (((0,), (0,)), ((), ())), preferred_element_type=jnp.float32
-            )
-        )
-    return jnp.concatenate(parts, axis=1)
+    for index in range(reps):
+        skip = max(index * block - (width - block), 0)
+        if skip < block:
+            parts.append(blocks[index, ..., skip:])
+    return jnp.concatenate(parts, axis=-1).astype(jnp.float32)
+
+
+def sum_all(grad):
+    part = lax.psum_scatter(grad, ("shard", "rep"), scatter_dimension=0, tiled=True)
+    return lax.all_gather(part, "rep", axis=0, tiled=True)
 
 
 def right_product(left, right):
@@ -104,6 +144,11 @@
     local_groups = joined_width // ((group_index + 2) * HEAD_SIZE)
     heads_width = output_weight.shape[2]
     hidden_width = down_weight.shape[2]
+    reps = lax.axis_size("rep")
+    block = -(-hidden_width // (reps * LANES)) * LANES
+    first_owned = lax.axis_index("rep") * block
+    first_unit = jnp.minimum(first_owned, hidden_width - block)
+    owned = first_unit + jnp.arange(block, dtype=jnp.int32)[None, :] >= first_owned
     root = math.sqrt(HEAD_SIZE)
     own_pos = place * span + jnp.arange(span, dtype=jnp.int32)
     all_pos = jnp.arange(length, dtype=jnp.int32)
@@ -121,13 +166,14 @@
     residual_state = x_in.astype(jnp.float32).reshape(rows, width)
     saved = []
     for index in range(LAYERS):
-        gathered = (
-            lax.all_gather(query_key_value_weight[index], "shard", axis=0, tiled=True),
-            lax.all_gather(output_weight[index], "shard", axis=0, tiled=True),
-            lax.all_gather(feedforward_entry_matrix[index], "shard", axis=0, tiled=True),
-            lax.all_gather(down_weight[index], "shard", axis=0, tiled=True),
-        )
-        full_qkv, full_out, full_gate_up, full_down = gathered
+        full_qkv, full_out, part_gate_up, part_down = layer_weights(
+            query_key_value_weight[index],
+            output_weight[index],
+            feedforward_entry_matrix[index],
+            down_weight[index],
+            first_unit,
+            block,
+        )
         gains = norm_gains[index].astype(jnp.float32)
         scale_one = norm_scale(residual_state)
         first_normed = (residual_state * scale_one * gains[0]).astype(jnp.bfloat16)
@@ -154,16 +200,10 @@
         middle_state = residual_state + lax.psum(right_product(mixed_output, full_out), "tp")
         scale_two = norm_scale(middle_state)
         rescaled_after_attention = (middle_state * scale_two * gains[1]).astype(jnp.bfloat16)
-        swiglu_input_pair = jnp.einsum(
-            "rd,dcf->rcf",
-            rescaled_after_attention,
-            full_gate_up,
-            preferred_element_type=jnp.float32,
-        )
-        hidden_state = (jax.nn.silu(swiglu_input_pair[:, 0]) * swiglu_input_pair[:, 1]).astype(
-            jnp.bfloat16
-        )
-        kept = None
+        plane_rows = lax.all_gather(rescaled_after_attention, "rep", axis=0, tiled=True)
+        gate = jnp.dot(plane_rows, part_gate_up[:, :block], preferred_element_type=jnp.float32)
+        upper = jnp.dot(plane_rows, part_gate_up[:, block:], preferred_element_type=jnp.float32)
+        hidden_state = jnp.where(owned, jax.nn.silu(gate) * upper, 0.0).astype(jnp.bfloat16)
         saved.append(
             (
                 residual_state,
@@ -176,16 +216,23 @@
                 mixed_output,
                 middle_state,
                 scale_two,
-                rescaled_after_attention,
-                swiglu_input_pair,
+                plane_rows,
+                gate,
+                upper,
                 hidden_state,
-                kept,
+                full_qkv,
+                full_out,
+                part_gate_up,
+                part_down,
             )
         )
-        residual_state = middle_state + lax.psum(right_product(hidden_state, full_down), "tp")
+        residual_state = middle_state + plane_sum(right_product(hidden_state, part_down))
     out_act = residual_state.astype(jnp.bfloat16).reshape(seqs, span, width)
     flow = grad_out.astype(jnp.float32).reshape(rows, width)
-    pieces = [None] * LAYERS
+    gate_pieces = [None] * LAYERS
+    down_pieces = [None] * LAYERS
+    qkv_pieces = [None] * LAYERS
+    out_pieces = [None] * LAYERS
     gain_grads = [None] * LAYERS
     bias_grads = [None] * LAYERS
     for index in reversed(range(LAYERS)):
@@ -200,30 +247,28 @@
             mixed_output,
             middle_state,
             scale_two,
-            rescaled_after_attention,
-            swiglu_input_pair,
+            plane_rows,
+            gate,
+            upper,
             hidden_state,
-            kept,
+            full_qkv,
+            full_out,
+            part_gate_up,
+            part_down,
         ) = saved[index]
-        full_qkv, full_out, full_gate_up, full_down = (
-            lax.all_gather(query_key_value_weight[index], "shard", axis=0, tiled=True),
-            lax.all_gather(output_weight[index], "shard", axis=0, tiled=True),
-            lax.all_gather(feedforward_entry_matrix[index], "shard", axis=0, tiled=True),
-            lax.all_gather(down_weight[index], "shard", axis=0, tiled=True),
-        )
         gains = norm_gains[index].astype(jnp.float32)
         down_grad = flow.astype(jnp.bfloat16)
-        hidden_grad = jnp.dot(down_grad, full_down, preferred_element_type=jnp.float32)
-        gate = swiglu_input_pair[:, 0]
-        upper = swiglu_input_pair[:, 1]
+        plane_grad = lax.all_gather(down_grad, "rep", axis=0, tiled=True)
+        hidden_grad = jnp.dot(plane_grad, part_down, preferred_element_type=jnp.float32)
         sigmoid = jax.nn.sigmoid(gate)
         gate_grad = hidden_grad * upper * (sigmoid + gate * sigmoid * (1.0 - sigmoid))
         up_grad = hidden_grad * (gate * sigmoid)
-        gate_up_grad = jnp.stack([gate_grad, up_grad], axis=1).astype(jnp.bfloat16)
-        normed_two_part = jnp.einsum(
-            "rcf,dcf->rd", gate_up_grad, full_gate_up, preferred_element_type=jnp.float32
-        )
-        normed_two_grad = lax.psum(normed_two_part, "tp")
+        gate_grad = jnp.where(owned, gate_grad, 0.0).astype(jnp.bfloat16)
+        up_grad = jnp.where(owned, up_grad, 0.0).astype(jnp.bfloat16)
+        normed_two_grad = plane_sum(
+            right_product(gate_grad, part_gate_up[:, :block])
+            + right_product(up_grad, part_gate_up[:, block:])
+        )
         middle_grad, gain_two = norm_back(middle_state, scale_two, gains[1], normed_two_grad)
         middle_grad = flow + middle_grad
         out_grad = middle_grad.astype(jnp.bfloat16)
@@ -275,26 +320,22 @@
         input_grad, gain_one = norm_back(residual_state, scale_one, gains[0], normed_one_grad)
         gain_grads[index] = jnp.stack([gain_one, gain_two])
         flow = middle_grad + input_grad
-        pairs = (
-            (first_normed, joined_grad),
-            (out_grad, mixed_output),
-            (rescaled_after_attention, gate_up_grad.reshape(rows, 2 * hidden_width)),
-            (down_grad, hidden_state),
-        )
-        pieces[index] = lax.psum_scatter(
-            weight_terms(pairs).astype(jnp.bfloat16), "shard", scatter_dimension=0, tiled=True
-        ).astype(jnp.float32)
-    stacked = jnp.stack(pieces)
-    summed = lax.psum(stacked.astype(jnp.bfloat16), "rep").astype(jnp.float32)
-    gains_total, bias_total = lax.psum(
-        (jnp.stack(gain_grads), jnp.stack(bias_grads)), ("rep", "shard")
-    )
-    second = joined_width + heads_width
-    third = second + 2 * hidden_width
-    grad_qkv = summed[:, :, :joined_width]
-    grad_out_proj = summed[:, :, joined_width:second]
-    grad_gate_up = summed[:, :, second:third].reshape(LAYERS, summed.shape[1], 2, hidden_width)
-    grad_down = summed[:, :, third:]
+        gate_pieces[index] = spread_block(
+            jnp.stack([left_product(plane_rows, gate_grad), left_product(plane_rows, up_grad)], 1)
+        )
+        down_pieces[index] = spread_block(left_product(plane_grad, hidden_state))
+        qkv_pieces[index] = sum_all(left_product(first_normed, joined_grad))
+        out_pieces[index] = sum_all(left_product(out_grad, mixed_output))
+    grad_gate_up = jnp.stack([join_blocks(g, hidden_width) for g in gate_pieces])
+    grad_down = jnp.stack([join_blocks(g, hidden_width) for g in down_pieces])
+    grad_qkv = jnp.stack(qkv_pieces).astype(jnp.float32)
+    grad_out_proj = jnp.stack(out_pieces).astype(jnp.float32)
+    bias = jnp.stack(bias_grads)
+    slots = jnp.arange(lax.axis_size("tp"), dtype=jnp.int32)[:, None, None] == lax.axis_index("tp")
+    bias_slots = jnp.where(slots, bias[None], 0.0)
+    gains_own = jnp.where(lax.axis_index("tp") == 0, jnp.stack(gain_grads), 0.0)
+    gains_total, bias_slots = lax.psum((gains_own, bias_slots), ("rep", "shard", "tp"))
+    bias_total = lax.dynamic_index_in_dim(bias_slots, lax.axis_index("tp"), 0, keepdims=False)
     grad_input = flow.reshape(seqs, span, width)
     return (
         out_act,

time: 4130 us -> 2730 us (0.66)
  waiting for transfers between devices: 3290 us -> 1980 us
  other arithmetic: 179 us -> 104 us
    all_gather x8 -> x16, waiting for transfers between devices: 1480 us -> 913 us  [the longest x2 216 us: layer_weights(): lax.all_gather(gate_up_block.reshape(depth, 2 * block), 'shard', axis=0,...]
    reduce_scatter x2 -> x12, waiting for transfers between devices: 1420 us -> 928 us  [the longest x4 450 us: sum_all(): lax.psum_scatter(grad, ('shard', 'rep'), scatter_dimension=0, tiled=True)]
    psum x4, waiting for transfers between devices: 352 us -> 35.6 us  [plane_sum(): return lax.psum(part, 'tp').astype(jnp.float32)]
    concatenate x2 -> x0, other arithmetic: 62.7 us -> none  [weight_terms(): return jnp.concatenate(parts, axis=1)]
    unnamed x180 -> x207, local copies, waits for them, and re-layouts: 46.5 us -> 105 us
    dot_general x14 -> x16, matrix products: 192 us -> 142 us  [the longest x10 75.1 us: left_product(): lax.dot_general(left, right, (((0,), (0,)), ((), ())), preferred_element_...]
    all_gather x0 -> x4, blocking collectives: none -> 49.6 us  [sum_all(): return lax.all_gather(part, 'rep', axis=0, tiled=True)]
    dot_general x6 -> x10, matrix products: 46.2 us -> 85.5 us  [right_product(): lax.dot_general(left, right, (((1,), (1,)), ((), ())), preferred_element_...]
  transfers between devices with their start and end apart: 22 -> 39, of which waited for: 16 -> 35; matrix products, arithmetic and copies ran while one was open for 10% -> 12% of each run, Pallas kernels for 0% -> 0%
where the time goes in v1:
time: 2730 us
  waiting for transfers between devices  1980 us (73%)
  matrix products  299 us (11%)
  local copies, waits for them, and re-layouts  169 us (6%)
  blocking collectives  157 us (6%)
  other arithmetic  104 us (4%)
    reduce_scatter x4, waiting for transfers between devices, sum_all(): lax.psum_scatter(grad, ('shard', 'rep'), scatter_dimension=0, tiled=True)  450 us
    reduce_scatter x4, waiting for transfers between devices, spread_block(): part = lax.psum_scatter(grad, 'shard', scatter_dimension=0, tiled=True)  260 us
    reduce_scatter x4, waiting for transfers between devices, plane_sum(): lax.psum_scatter(terms.astype(jnp.bfloat16), 'rep', scatter_dimension=0,...  218 us
    all_gather x2, waiting for transfers between devices, layer_weights(): lax.all_gather(gate_up_block.reshape(depth, 2 * block), 'shard', axis=0,...  216 us
    all_gather x4, waiting for transfers between devices, spread_block(): return lax.all_gather(part, 'rep', axis=0, tiled=False)  215 us
    all_gather x4, waiting for transfers between devices, whole(): return lax.all_gather(rows, ('shard', 'rep'), axis=0, tiled=True)  150 us
    all_gather x2, waiting for transfers between devices, body(): plane_grad = lax.all_gather(down_grad, 'rep', axis=0, tiled=True)  115 us
    all_gather x2, waiting for transfers between devices, body(): lax.all_gather(rescaled_after_attention, 'rep', axis=0, tiled=True)  115 us
  transfers between devices with their start and end apart: 39, of which 35 were waited for; matrix products, arithmetic and copies ran while one was open for 12% of the time, Pallas kernels for 0%

profile of v1, /device:TPU:0, one launch (start us, length us, event | category | flops | bytes accessed | tf_op | source)
XLA Modules:
  0.0 2727.2 jit_solution(13959589676479864081)
XLA Ops:
  20.7 62.1 %all-gather.40.cloned.1.call-done = bf16[1,1536,1024]{2,1,0:T(8,128)(2,1)} async-done(((bf16[1,96,1024]{2,1,0:T(8,128)(2,1)}), bf16[1,1536,1024]{2,1,0:T(8,128)(2,1)}) %all-gather.40.cloned.1.call-update) | async-done | bytes 3145744 | tf_op jit(solution)/shard_map/all_gather | solution.py:82
  96.6 15.0 all_gather.86
  111.6 17.5 all-gather.1
  154.6 11.1 fusion.179
  188.6 114.3 %all-gather.32.cloned.1.call-done = bf16[1536,2304]{1,0:T(8,128)(2,1)} async-done(((bf16[384,2304]{1,0:T(8,128)(2,1)}), bf16[1536,2304]{1,0:T(8,128)(2,1)}) %all-gather.32.cloned.1.call-update) | async-done | bytes 7077904 | tf_op jit(solution)/shard_map/all_gather | solution.py:89
  302.9 57.3 %all-gather.30.cloned.1.call-done = bf16[1536,1536]{1,0:T(8,128)(2,1)} async-done(((bf16[384,1536]{1,0:T(8,128)(2,1)}), bf16[1536,1536]{1,0:T(8,128)(2,1)}) %all-gather.30.cloned.1.call-update) | async-done | bytes 4718608 | tf_op jit(solution)/shard_map/all_gather | solution.py:203
  381.4 50.6 %all-gather.44.cloned.1.call-done = bf16[1,1536,1152]{2,1,0:T(8,128)(2,1)} async-done(((bf16[1,384,1152]{2,1,0:T(8,128)(2,1)}), bf16[1,1536,1152]{2,1,0:T(8,128)(2,1)}) %all-gather.44.cloned.1.call-update) | async-done | bytes 3538960 | tf_op jit(solution)/shard_map/all_gather | solution.py:90
  442.6 55.5 %reduce-scatter.21.cloned.1.call-done = bf16[384,1536]{1,0:T(8,128)(2,1)} async-done(((bf16[1536,1536]{1,0:T(8,128)(2,1)}), bf16[384,1536]{1,0:T(8,128)(2,1)}) %reduce-scatter.21.cloned.1.call-update) | async-done | bytes 1179664 | tf_op jit(solution)/shard_map/reduce_scatter | solution.py:95
  501.6 16.4 all-reduce.12.cloned.1.call-done
  521.0 69.3 %all-gather.46.cloned.1.call-done = bf16[1,1536,1024]{2,1,0:T(8,128)(2,1)} async-done(((bf16[1,96,1024]{2,1,0:T(8,128)(2,1)}), bf16[1,1536,1024]{2,1,0:T(8,128)(2,1)}) %all-gather.46.cloned.1.call-update) | async-done | bytes 3145744 | tf_op jit(solution)/shard_map/all_gather | solution.py:82
  598.5 16.0 all_gather.93
  614.6 17.9 all-gather.5
  661.4 18.7 all-reduce.14.cloned.1.call-done
  687.9 101.3 %all-gather.36.cloned.1.call-done = bf16[1536,2304]{1,0:T(8,128)(2,1)} async-done(((bf16[384,2304]{1,0:T(8,128)(2,1)}), bf16[1536,2304]{1,0:T(8,128)(2,1)}) %all-gather.36.cloned.1.call-update) | async-done | bytes 7077904 | tf_op jit(solution)/shard_map/all_gather | solution.py:89
  789.3 57.5 %all-gather.34.cloned.1.call-done = bf16[1536,1536]{1,0:T(8,128)(2,1)} async-done(((bf16[384,1536]{1,0:T(8,128)(2,1)}), bf16[1536,1536]{1,0:T(8,128)(2,1)}) %all-gather.34.cloned.1.call-update) | async-done | bytes 4718608 | tf_op jit(solution)/shard_map/all_gather | solution.py:203
  866.1 51.9 %all-gather.50.cloned.1.call-done = bf16[1,1536,1152]{2,1,0:T(8,128)(2,1)} async-done(((bf16[1,384,1152]{2,1,0:T(8,128)(2,1)}), bf16[1,1536,1152]{2,1,0:T(8,128)(2,1)}) %all-gather.50.cloned.1.call-update) | async-done | bytes 3538960 | tf_op jit(solution)/shard_map/all_gather | solution.py:90
  918.0 57.1 %all-gather.52.cloned.1.call-done = bf16[1,1536,1536]{2,1,0:T(8,128)(2,1)} async-done(((bf16[1,384,1536]{2,1,0:T(8,128)(2,1)}), bf16[1,1536,1536]{2,1,0:T(8,128)(2,1)}) %all-gather.52.cloned.1.call-update) | async-done | bytes 4718608 | tf_op jit(solution)/shard_map/all_gather | solution.py:261
  975.2 15.7 select_convert_fusion.2
  990.8 13.3 fusion.37
  1004.1 11.5 add_convert_fusion.1
  1015.7 56.9 %reduce-scatter.25.cloned.1.call-done = bf16[384,1536]{1,0:T(8,128)(2,1)} async-done(((bf16[1536,1536]{1,0:T(8,128)(2,1)}), bf16[384,1536]{1,0:T(8,128)(2,1)}) %reduce-scatter.25.cloned.1.call-update) | async-done | bytes 1179664 | tf_op jit(solution)/shard_map/reduce_scatter | solution.py:95
  1073.2 19.2 all-reduce.16.cloned.1.call-done
  1140.2 20.6 reduce-scatter.27.cloned.1.call-done
  1170.7 18.1 all-reduce.18.cloned.1.call-done
  1194.3 57.9 %all-gather.38.cloned.1.call-done = bf16[1536,1536]{1,0:T(8,128)(2,1)} async-done(((bf16[384,1536]{1,0:T(8,128)(2,1)}), bf16[1536,1536]{1,0:T(8,128)(2,1)}) %all-gather.38.cloned.1.call-update) | async-done | bytes 4718608 | tf_op jit(solution)/shard_map/all_gather | solution.py:261
  1252.2 13.8 select_convert_fusion
  1287.0 56.9 %reduce-scatter.29.cloned.1.call-done = bf16[384,1536]{1,0:T(8,128)(2,1)} async-done(((bf16[1536,1536]{1,0:T(8,128)(2,1)}), bf16[384,1536]{1,0:T(8,128)(2,1)}) %reduce-scatter.29.cloned.1.call-update) | async-done | bytes 1179664 | tf_op jit(solution)/shard_map/reduce_scatter | solution.py:95
  1429.7 11.4 convolution_convert_fusion.6
  1473.6 73.6 %reduce-scatter.43.cloned.1.call-done = bf16[384,2,1152]{2,0,1:T(8,128)(2,1)} async-done(((bf16[1536,2,1152]{2,0,1:T(8,128)(2,1)}), bf16[384,2,1152]{2,0,1:T(8,128)(2,1)}) %reduce-scatter.43.cloned.1.call-update) | async-done | bytes 1769488 | tf_op jit(solution)/shard_map/reduce_scatter | solution.py:100
  1547.3 69.3 %reduce-scatter.45.cloned.1.call-done = bf16[384,1152]{1,0:T(8,128)(2,1)} async-done(((bf16[1536,1152]{1,0:T(8,128)(2,1)}), bf16[384,1152]{1,0:T(8,128)(2,1)}) %reduce-scatter.45.cloned.1.call-update) | async-done | bytes 884752 | tf_op jit(solution)/shard_map/reduce_scatter | solution.py:100
  1621.2 19.3 reduce-scatter.51.cloned.1.call-done
  1641.7 20.2 reduce-scatter.31.cloned.1.call-done
  1671.7 48.2 %reduce-scatter.23.cloned.1.call-done = bf16[384,1536]{1,0:T(8,128)(2,1)} async-done(((bf16[1536,1536]{1,0:T(8,128)(2,1)}), bf16[384,1536]{1,0:T(8,128)(2,1)}) %reduce-scatter.23.cloned.1.call-update) | async-done | bytes 1179664 | tf_op jit(solution)/shard_map/reduce_scatter | solution.py:95
  1729.1 117.2 %reduce-scatter.41.cloned.1.call-done = bf16[384,2,1152]{2,0,1:T(8,128)(2,1)} async-done(((bf16[1536,2,1152]{2,0,1:T(8,128)(2,1)}), bf16[384,2,1152]{2,0,1:T(8,128)(2,1)}) %reduce-scatter.41.cloned.1.call-update) | async-done | bytes 1769488 | tf_op jit(solution)/shard_map/reduce_scatter | solution.py:100
  1846.4 49.2 %all-gather.60.cloned.1.call-done = bf16[1536,1152]{1,0:T(8,128)(2,1)} async-done(((bf16[384,1152]{1,0:T(8,128)(2,1)}), bf16[1536,1152]{1,0:T(8,128)(2,1)}) %all-gather.60.cloned.1.call-update) | async-done | bytes 3538960 | tf_op jit(solution)/shard_map/all_gather | solution.py:101
  1901.1 129.0 %reduce-scatter.39.cloned.1.call-done = bf16[96,768]{1,0:T(8,128)(2,1)} async-done(((bf16[1536,768]{1,0:T(8,128)(2,1)}), bf16[96,768]{1,0:T(8,128)(2,1)}) %reduce-scatter.39.cloned.1.call-update) | async-done | bytes 147472 | tf_op jit(solution)/shard_map/reduce_scatter | solution.py:115
  2030.1 12.3 all_gather.103
  2042.3 124.3 %reduce-scatter.35.cloned.1.call-done = bf16[96,1024]{1,0:T(8,128)(2,1)} async-done(((bf16[1536,1024]{1,0:T(8,128)(2,1)}), bf16[96,1024]{1,0:T(8,128)(2,1)}) %reduce-scatter.35.cloned.1.call-update) | async-done | bytes 196624 | tf_op jit(solution)/shard_map/reduce_scatter | solution.py:115
  2166.6 14.1 all_gather.101
  2180.8 63.1 %all-gather.56.cloned.1.call-done = bf16[1536,2,1152]{2,0,1:T(8,128)(2,1)} async-done(((bf16[384,2,1152]{2,0,1:T(8,128)(2,1)}), bf16[1536,2,1152]{2,0,1:T(8,128)(2,1)}) %all-gather.56.cloned.1.call-update) | async-done | bytes 7077904 | tf_op jit(solution)/shard_map/all_gather | solution.py:101
  2253.0 39.7 %all-gather.58.cloned.1.call-done = bf16[1536,1152]{1,0:T(8,128)(2,1)} async-done(((bf16[384,1152]{1,0:T(8,128)(2,1)}), bf16[1536,1152]{1,0:T(8,128)(2,1)}) %all-gather.58.cloned.1.call-update) | async-done | bytes 3538960 | tf_op jit(solution)/shard_map/all_gather | solution.py:101
  2305.4 41.0 %all-reduce = (f32[2,2,1024]{2,1,0:T(2,128)}, f32[2,2,1536]{2,1,0:T(2,128)}) all-reduce(f32[2,2,1024]{2,1,0:T(2,128)} %broadcast_select_fusion, f32[2,2,1536]{2,1,0:T(2,128)} %maximum_select_fusion), channel_id=1, replica_groups=mesh['rep'=4,'shard'=4,'tp'=2] {'rep','shard','tp'}, use_global_device_ids=true, to_apply=%region_36.37 | all-reduce | flops 10240 | bytes 81920 | tf_op jit(solution)/shard_map/psum | solution.py:337
  2354.1 73.2 %reduce-scatter.37.cloned.1.call-done = bf16[96,768]{1,0:T(8,128)(2,1)} async-done(((bf16[1536,768]{1,0:T(8,128)(2,1)}), bf16[96,768]{1,0:T(8,128)(2,1)}) %reduce-scatter.37.cloned.1.call-update) | async-done | bytes 147472 | tf_op jit(solution)/shard_map/reduce_scatter | solution.py:115
  2427.2 11.1 all_gather.102
  2439.9 123.5 %reduce-scatter.33.cloned.1.call-done = bf16[96,1024]{1,0:T(8,128)(2,1)} async-done(((bf16[1536,1024]{1,0:T(8,128)(2,1)}), bf16[96,1024]{1,0:T(8,128)(2,1)}) %reduce-scatter.33.cloned.1.call-update) | async-done | bytes 196624 | tf_op jit(solution)/shard_map/reduce_scatter | solution.py:115
  2563.4 12.1 all_gather.100
  2577.4 63.1 %all-gather.54.cloned.1.call-done = bf16[1536,2,1152]{2,0,1:T(8,128)(2,1)} async-done(((bf16[384,2,1152]{2,0,1:T(8,128)(2,1)}), bf16[1536,2,1152]{2,0,1:T(8,128)(2,1)}) %all-gather.54.cloned.1.call-update) | async-done | bytes 7077904 | tf_op jit(solution)/shard_map/all_gather | solution.py:101
  2655.7 63.9 %copy.163 = f32[2,384,2,4480]{3,2,1,0:T(2,128)} copy(f32[2,384,2,4480]{3,1,2,0:T(8,128)} %maximum_convert_fusion) | data formatting | bytes 55050240
  (442 shorter events, 456.7 us)
Async XLA Ops:
  8.0 74.8 %all-gather.40.cloned.1.call-start = ((), (), s32[]{:S(2)}) async-start(), calls=%async_computation.41 | async-start | bytes 3342336 | tf_op jit(solution)/shard_map/all_gather | solution.py:82
  11.3 138.5 %all-gather.42.cloned.1.call-start = ((), (), s32[]{:S(2)}) async-start(), calls=%async_computation.42 | async-start | bytes 2506752 | tf_op jit(solution)/shard_map/all_gather | solution.py:82
  13.0 163.5 %all-reduce.10.cloned.1.call-start = ((), (), s32[]{:S(2)}) async-start(), calls=%async_computation.16 | async-start | bytes 4718592 | tf_op jit(solution)/shard_map/psum | solution.py:200
  13.7 165.4 %copy-start.64 = (f32[1536]{0:T(1024)}, f32[1536]{0:T(1024)S(1)}, u32[]{:S(2)}) copy-start(f32[1536]{0:T(1024)S(1)} %get-tuple-element.50) | copy-start | bytes 18436
  14.8 80.9 %copy-start.20 = (f32[1,384,1,64]{3,1,2,0:T(8,128)}, f32[1,384,1,64]{3,1,2,0:T(8,128)S(1)}, u32[]{:S(2)}) copy-start(f32[1,384,1,64]{3,1,2,0:T(8,128)S(1)} %get-tuple-element.117) | copy-start | bytes 294916
  154.2 148.6 %all-gather.32.cloned.1.call-start = ((), (), s32[]{:S(2)}) async-start(), calls=%async_computation.18 | async-start | bytes 8847360 | tf_op jit(solution)/shard_map/all_gather | solution.py:89
  176.4 183.8 %all-gather.30.cloned.1.call-start = ((), (), s32[]{:S(2)}) async-start(), calls=%async_computation.17 | async-start | bytes 5898240 | tf_op jit(solution)/shard_map/all_gather | solution.py:203
  178.5 339.5 %copy-start.4 = (f32[384,1536]{1,0:T(8,128)}, f32[384,1536]{1,0:T(8,128)S(1)}, u32[]{:S(2)}) copy-start(f32[384,1536]{1,0:T(8,128)S(1)} %get-tuple-element.67) | copy-start | bytes 7077892
  180.5 251.6 %all-gather.44.cloned.1.call-start = ((), (), s32[]{:S(2)}) async-start(), calls=%async_computation.43 | async-start | bytes 4423680 | tf_op jit(solution)/shard_map/all_gather | solution.py:90
  188.1 310.1 %reduce-scatter.21.cloned.1.call-start = ((), (), s32[]{:S(2)}) async-start(), calls=%async_computation.19 | async-start | bytes 5898240 | tf_op jit(solution)/shard_map/reduce_scatter | solution.py:95
  442.6 75.4 %all-reduce.12.cloned.1.call-start = ((), (), s32[]{:S(2)}) async-start(), calls=%async_computation.20 | async-start | bytes 2359296 | tf_op jit(solution)/shard_map/psum | solution.py:96
  498.2 92.1 %all-gather.46.cloned.1.call-start = ((), (), s32[]{:S(2)}) async-start(), calls=%async_computation.44 | async-start | bytes 3342336 | tf_op jit(solution)/shard_map/all_gather | solution.py:82
  499.8 155.5 %all-gather.48.cloned.1.call-start = ((), (), s32[]{:S(2)}) async-start(), calls=%async_computation.45 | async-start | bytes 2506752 | tf_op jit(solution)/shard_map/all_gather | solution.py:82
  501.5 178.6 %all-reduce.14.cloned.1.call-start = ((), (), s32[]{:S(2)}) async-start(), calls=%async_computation.21 | async-start | bytes 4718592 | tf_op jit(solution)/shard_map/psum | solution.py:200
  659.8 129.4 %all-gather.36.cloned.1.call-start = ((), (), s32[]{:S(2)}) async-start(), calls=%async_computation.23 | async-start | bytes 8847360 | tf_op jit(solution)/shard_map/all_gather | solution.py:89
  661.4 185.4 %all-gather.34.cloned.1.call-start = ((), (), s32[]{:S(2)}) async-start(), calls=%async_computation.22 | async-start | bytes 5898240 | tf_op jit(solution)/shard_map/all_gather | solution.py:203
  682.9 412.2 %copy-start.6 = (f32[384,1536]{1,0:T(8,128)}, f32[384,1536]{1,0:T(8,128)S(1)}, u32[]{:S(2)}) copy-start(f32[384,1536]{1,0:T(8,128)S(1)} %get-tuple-element.63) | copy-start | bytes 7077892
  684.5 233.6 %all-gather.50.cloned.1.call-start = ((), (), s32[]{:S(2)}) async-start(), calls=%async_computation.46 | async-start | bytes 4423680 | tf_op jit(solution)/shard_map/all_gather | solution.py:90
  687.1 288.1 %all-gather.52.cloned.1.call-start = ((), (), s32[]{:S(2)}) async-start(), calls=%async_computation.47 | async-start | bytes 5898240 | tf_op jit(solution)/shard_map/all_gather | solution.py:261
  687.7 384.9 %reduce-scatter.25.cloned.1.call-start = ((), (), s32[]{:S(2)}) async-start(), calls=%async_computation.25 | async-start | bytes 5898240 | tf_op jit(solution)/shard_map/reduce_scatter | solution.py:95
  1015.6 76.8 %all-reduce.16.cloned.1.call-start = ((), (), s32[]{:S(2)}) async-start(), calls=%async_computation.26 | async-start | bytes 2359296 | tf_op jit(solution)/shard_map/psum | solution.py:96
  1072.6 66.4 %reduce-scatter.49.cloned.1.call-start = ((), (), s32[]{:S(2)}) async-start(), calls=%async_computation.52 | async-start | bytes 491520
  1117.0 43.8 %reduce-scatter.27.cloned.1.call-start = ((), (), s32[]{:S(2)}) async-start(), calls=%async_computation.27 | async-start | bytes 491520 | tf_op jit(solution)/shard_map/reduce_scatter | solution.py:303
  1133.0 55.8 %all-reduce.18.cloned.1.call-start = ((), (), s32[]{:S(2)}) async-start(), calls=%async_computation.28 | async-start | bytes 2359296 | tf_op jit(solution)/shard_map/psum | solution.py:317
  1170.6 81.6 %all-gather.38.cloned.1.call-start = ((), (), s32[]{:S(2)}) async-start(), calls=%async_computation.29 | async-start | bytes 5898240 | tf_op jit(solution)/shard_map/all_gather | solution.py:261
  1194.0 149.9 %reduce-scatter.29.cloned.1.call-start = ((), (), s32[]{:S(2)}) async-start(), calls=%async_computation.30 | async-start | bytes 5898240 | tf_op jit(solution)/shard_map/reduce_scatter | solution.py:95
  1286.9 100.4 %all-reduce.20.cloned.1.call-start = ((), (), s32[]{:S(2)}) async-start(), calls=%async_computation.31 | async-start | bytes 2359296 | tf_op jit(solution)/shard_map/psum | solution.py:96
  1343.9 118.9 %reduce-scatter.47.cloned.1.call-start = ((), (), s32[]{:S(2)}) async-start(), calls=%async_computation.40 | async-start | bytes 4423680 | tf_op jit(solution)/shard_map/reduce_scatter | solution.py:100
  1354.7 192.5 %reduce-scatter.43.cloned.1.call-start = ((), (), s32[]{:S(2)}) async-start(), calls=%async_computation.38 | async-start | bytes 8847360 | tf_op jit(solution)/shard_map/reduce_scatter | solution.py:100
  1376.1 240.5 %reduce-scatter.45.cloned.1.call-start = ((), (), s32[]{:S(2)}) async-start(), calls=%async_computation.39 | async-start | bytes 4423680 | tf_op jit(solution)/shard_map/reduce_scatter | solution.py:100
  1387.3 253.3 %reduce-scatter.51.cloned.1.call-start = ((), (), s32[]{:S(2)}) async-start(), calls=%async_computation.53 | async-start | bytes 491520
  1413.3 248.6 %reduce-scatter.31.cloned.1.call-start = ((), (), s32[]{:S(2)}) async-start(), calls=%async_computation.32 | async-start | bytes 491520 | tf_op jit(solution)/shard_map/reduce_scatter | solution.py:303
  1429.4 290.4 %reduce-scatter.23.cloned.1.call-start = ((), (), s32[]{:S(2)}) async-start(), calls=%async_computation.24 | async-start | bytes 5898240 | tf_op jit(solution)/shard_map/reduce_scatter | solution.py:95
  1441.1 405.2 %reduce-scatter.41.cloned.1.call-start = ((), (), s32[]{:S(2)}) async-start(), calls=%async_computation.37 | async-start | bytes 8847360 | tf_op jit(solution)/shard_map/reduce_scatter | solution.py:100
  1462.7 432.8 %all-gather.60.cloned.1.call-start = ((), (), s32[]{:S(2)}) async-start(), calls=%async_computation.51 | async-start | bytes 4423680 | tf_op jit(solution)/shard_map/all_gather | solution.py:101
  1463.3 566.8 %reduce-scatter.39.cloned.1.call-start = ((), (), s32[]{:S(2)}) async-start(), calls=%async_computation.36 | async-start | bytes 2506752 | tf_op jit(solution)/shard_map/reduce_scatter | solution.py:115
  1468.5 698.1 %reduce-scatter.35.cloned.1.call-start = ((), (), s32[]{:S(2)}) async-start(), calls=%async_computation.34 | async-start | bytes 3342336 | tf_op jit(solution)/shard_map/reduce_scatter | solution.py:115
  1473.6 143.2 %copy-start.42 = (bf16[1,1536,1,128]{3,1,2,0:T(8,128)(2,1)S(1)}, bf16[1,1536,1,128]{3,1,2,0:T(8,128)(2,1)}, u32[]{:S(2)}) copy-start(bf16[1,1536,1,128]{3,1,2,0:T(8,128)(2,1)} %copy-done.41) | copy-start | bytes 1179652
  1473.6 143.2 %copy-start.55 = (f32[384,128]{0,1:T(8,128)S(1)}, f32[384,128]{0,1:T(8,128)}, u32[]{:S(2)}) copy-start(f32[384,128]{0,1:T(8,128)} %copy-done.54) | copy-start | bytes 589828
  1473.6 770.3 %all-gather.56.cloned.1.call-start = ((), (), s32[]{:S(2)}) async-start(), calls=%async_computation.49 | async-start | bytes 8847360 | tf_op jit(solution)/shard_map/all_gather | solution.py:101
  1547.3 745.4 %all-gather.58.cloned.1.call-start = ((), (), s32[]{:S(2)}) async-start(), calls=%async_computation.50 | async-start | bytes 4423680 | tf_op jit(solution)/shard_map/all_gather | solution.py:101
  1616.7 684.6 %all-reduce.22.cloned.1.call-start = ((), (), s32[]{:S(2)}) async-start(), calls=%async_computation.54 | async-start | bytes 4718592 | tf_op jit(solution)/shard_map/psum | solution.py:96
  1719.9 707.3 %reduce-scatter.37.cloned.1.call-start = ((), (), s32[]{:S(2)}) async-start(), calls=%async_computation.35 | async-start | bytes 2506752 | tf_op jit(solution)/shard_map/reduce_scatter | solution.py:115
  1724.0 839.4 %reduce-scatter.33.cloned.1.call-start = ((), (), s32[]{:S(2)}) async-start(), calls=%async_computation.33 | async-start | bytes 3342336 | tf_op jit(solution)/shard_map/reduce_scatter | solution.py:115
  1729.0 117.3 %copy-start.71 = (f32[1536]{0:T(1024)S(1)}, f32[1536]{0:T(1024)}, u32[]{:S(2)}) copy-start(f32[1536]{0:T(1024)} %get-tuple-element.44) | copy-start | bytes 18436
  1729.0 911.4 %all-gather.54.cloned.1.call-start = ((), (), s32[]{:S(2)}) async-start(), calls=%async_computation.48 | async-start | bytes 8847360 | tf_op jit(solution)/shard_map/all_gather | solution.py:101
  2351.1 87.2 %copy-start.49 = (bf16[384,768]{1,0:T(8,128)(2,1)S(1)}, bf16[384,768]{1,0:T(8,128)(2,1)}, u32[]{:S(2)}) copy-start(bf16[384,768]{1,0:T(8,128)(2,1)} %all_gather.103) | copy-start | bytes 1769476
  2354.1 221.5 %copy-start.47 = (bf16[384,1024]{1,0:T(8,128)(2,1)S(1)}, bf16[384,1024]{1,0:T(8,128)(2,1)}, u32[]{:S(2)}) copy-start(bf16[384,1024]{1,0:T(8,128)(2,1)} %all_gather.101) | copy-start | bytes 2359300
  (85 other events, 1184.5 us)
Sparse Core Ops, SparseCore 0:
  12.2 70.5 all-gather.39
  86.2 63.5 all-gather.41
  154.4 20.1 all-reduce.9
  498.3 19.6 all-reduce.11
  521.2 69.0 all-gather.45
  593.5 61.7 all-gather.47
  660.0 20.1 all-reduce.13
  1072.7 19.6 all-reduce.15
  1170.7 18.0 all-reduce.17
  1344.0 19.6 all-reduce.19
  1720.0 21.8 all-reduce.21
Sparse Core Ops, SparseCore 1:
  176.4 126.4 all-gather.31
  305.2 55.0 all-gather.29
  362.2 69.8 all-gather.43
  442.7 55.4 reduce-scatter.20
  662.8 126.4 all-gather.35
  791.7 55.0 all-gather.33
  848.2 69.8 all-gather.49
  919.7 55.4 all-gather.51
  1015.7 56.8 reduce-scatter.24
  1117.1 21.9 reduce-scatter.48
  1141.8 18.9 reduce-scatter.26
  1194.1 58.0 all-gather.37
  1287.0 56.8 reduce-scatter.28
  1354.8 66.5 reduce-scatter.46
  1423.7 123.5 reduce-scatter.42
  1549.6 67.0 reduce-scatter.44
  1619.5 21.0 reduce-scatter.50
  1642.8 19.0 reduce-scatter.30
  1664.8 55.0 reduce-scatter.22
  1722.8 123.4 reduce-scatter.40
  1848.0 47.5 all-gather.59
  1900.3 129.7 reduce-scatter.38
  2035.5 131.1 reduce-scatter.34
  2168.5 75.3 all-gather.55
  2245.6 47.0 all-gather.57
  2298.2 129.0 reduce-scatter.36
  2432.2 131.1 reduce-scatter.32
  2565.1 75.3 all-gather.53
